TPU v7x, 32 devices: a whole 2x2x4 slice. The times are simulated.
32 devices in a mesh: row: 4 (over y, core), col: 8 (over z, x).
Axes of the slice: x: 2, y: 2, z: 4, core: 2. Of those that a mesh axis runs over, the one named last changes fastest.
Arguments:
- points: float32 [1280, 128], P(('row', 'col')), may hold values from -6 to 6
- source_ids: int32 [1280], P(('row', 'col')), may hold values from 0 to 63
- source_shift: float32 [64, 128], replicated, may hold values from -4 to 4
- noise_level: float32 [64], replicated, may hold values from 0.1 to 1
- weight_in: float32 [128, 256], replicated, may hold values from -0.5 to 0.5
- bias_in: float32 [256], replicated, may hold values from -3 to 3
- weight_out: float32 [256, 32], replicated, may hold values from -0.375 to 0.375
- inverse_scale: float32 [32], replicated, may hold values from 0.15 to 0.6
- frequency: float32 [32, 256], replicated, may hold values from -5 to 5
- phase_shift: float32 [256], replicated, may hold values from -3.140625 to 3.140625
- solution: float32 [1280, 128], P(('row', 'col')), may hold values from -6 to 6
- residual: float32 [1280, 128], P(('row', 'col')), may hold values from -6 to 6
- direction: float32 [1280, 128], P(('row', 'col')), may hold values from -6 to 6
- prior_product: float32 [128], replicated, may hold values from 80 to 640
Outputs:
- new_solution: float32 [1280, 128], P(('row', 'col'))
- new_residual: float32 [1280, 128], P(('row', 'col'))
- new_direction: float32 [1280, 128], P(('row', 'col'))
- new_product: float32 [128], replicated
All inputs are finite; a program needn't handle non-finite values.
Results may differ from a plain program's by a relative error of at most 0.00024.
Values sent between devices are 32-bit elements; how exact they have to be, the bound alone decides.
A program may use at most 64 MiB of HBM per device.

v0:
```python
import functools
import math

import jax
import jax.numpy as jnp
from jax import lax
from jax.experimental import pallas as pl
from jax.experimental.pallas import tpu as pltpu
from jax.sharding import PartitionSpec as P

HIGH = lax.Precision.HIGHEST
MESH = pl.DeviceIdType.MESH
VMEM = pl.BlockSpec(memory_space=pltpu.VMEM)


def mm(a, b, ca=1, cb=0):
    return lax.dot_general(
        a, b, (((ca,), (cb,)), ((), ())), precision=HIGH, preferred_element_type=jnp.float32
    )


def cosine(x):
    n = jnp.floor(x * 0.3183098861837907 + 0.5)
    r = ((x - n * 3.140625) - n * 9.67502593994140625e-4) - n * 1.509957990978376432e-7
    half = n * 0.5
    sign = 1.0 - 4.0 * (half - jnp.floor(half))
    z = r * r
    p = 2.08767569878681e-9
    for c in (
        -2.75573192239859e-7,
        2.48015873015873e-5,
        -1.38888888888889e-3,
        4.16666666666667e-2,
        -0.5,
        1.0,
    ):
        p = p * z + c
    return sign * p


def invert_block(m):
    size = m.shape[0]
    m = m.reshape(size // 8, 8, size)
    shape = m.shape
    lane = lax.broadcasted_iota(jnp.int32, (8, size), 1)
    sub = lax.broadcasted_iota(jnp.int32, (8, size), 0)
    for k in range(0, size, 4):
        group, off = divmod(k, 8)
        cols = [jnp.broadcast_to(m[:, :, k + j : k + j + 1], shape) for j in range(4)]
        own = m[group]
        rows = [jnp.broadcast_to(own[off + i : off + i + 1, :], (8, size)) for i in range(4)]

        def at(i, j):
            return jnp.broadcast_to(cols[j][group][off + i : off + i + 1, :], (8, size))

        a00, a01, a11 = at(0, 0), at(0, 1), at(1, 1)
        b00, b01, b10, b11 = at(0, 2), at(0, 3), at(1, 2), at(1, 3)
        d00, d01, d11 = at(2, 2), at(2, 3), at(3, 3)
        inv = 1.0 / (a00 * a11 - a01 * a01)
        e00, e01, e11 = a11 * inv, -a01 * inv, a00 * inv
        f00, f01 = e00 * b00 + e01 * b10, e00 * b01 + e01 * b11
        f10, f11 = e01 * b00 + e11 * b10, e01 * b01 + e11 * b11
        s00 = d00 - (b00 * f00 + b10 * f10)
        s01 = d01 - (b00 * f01 + b10 * f11)
        s11 = d11 - (b01 * f01 + b11 * f11)
        inv = 1.0 / (s00 * s11 - s01 * s01)
        t00, t01, t11 = s11 * inv, -s01 * inv, s00 * inv
        g00, g01 = f00 * t00 + f01 * t01, f00 * t01 + f01 * t11
        g10, g11 = f10 * t00 + f11 * t01, f10 * t01 + f11 * t11
        p00 = e00 + g00 * f00 + g01 * f01
        p01 = e01 + g00 * f10 + g01 * f11
        p11 = e11 + g10 * f10 + g11 * f11
        pivots = (
            (p00, p01, -g00, -g01),
            (p01, p11, -g10, -g11),
            (-g00, -g10, t00, t01),
            (-g01, -g11, t01, t11),
        )
        masks = [lane == k + j for j in range(4)]
        inside = (lane >= k) & (lane < k + 4)
        rows = [
            jnp.where(masks[j], 1.0, jnp.where(inside, 0.0, rows[j])) for j in range(4)
        ]
        scaled = [
            (pivots[i][0] * rows[0] + pivots[i][1] * rows[1])
            + (pivots[i][2] * rows[2] + pivots[i][3] * rows[3])
            for i in range(4)
        ]
        base = jnp.where(inside[None], 0.0, m)
        update = (cols[0] * scaled[0][None] + cols[1] * scaled[1][None]) + (
            cols[2] * scaled[2][None] + cols[3] * scaled[3][None]
        )
        m = base - update
        fixed = m[group]
        for i in range(4):
            fixed = jnp.where(sub == off + i, scaled[i], fixed)
        pieces = [fixed[None]]
        if group > 0:
            pieces.insert(0, m[:group])
        if group + 1 < size // 8:
            pieces.append(m[group + 1 :])
        m = jnp.concatenate(pieces, axis=0) if len(pieces) > 1 else pieces[0]
    return m.reshape(size, size)


def invert(a):
    size = a.shape[0]
    if size <= 128:
        return invert_block(a)
    h = size // 2
    top, cross, low = a[:h, :h], a[:h, h:], a[h:, h:]
    x = invert(top)
    y = mm(x, cross)
    z = invert(low - mm(cross, y, 0, 0))
    yz = mm(y, z)
    first = jnp.concatenate([x + mm(yz, y, 1, 1), -yz], axis=1)
    second = jnp.concatenate([-yz.T, z], axis=1)
    return jnp.concatenate([first, second], axis=0)


class Peers:
    def __init__(self, rows, cols):
        self.cols, self.count = cols, rows * cols
        self.me = lax.axis_index("row") * cols + lax.axis_index("col")

    def id(self, d):
        t = lax.rem(self.me + d, self.count)
        return t, {"row": t // self.cols, "col": lax.rem(t, self.cols)}

    def each(self, body):
        def turn(d, carry):
            body(*self.id(d))
            return carry

        lax.fori_loop(1, self.count, turn, 0)

    def greet(self):
        barrier = pltpu.get_barrier_semaphore()
        self.each(
            lambda t, dev: pl.semaphore_signal(barrier, inc=1, device_id=dev, device_id_type=MESH)
        )

    def meet(self):
        pl.semaphore_wait(pltpu.get_barrier_semaphore(), self.count - 1)

    def send(self, src, dst, send_sem, recv_sem, dev):
        pltpu.make_async_remote_copy(
            src_ref=src,
            dst_ref=dst,
            send_sem=send_sem,
            recv_sem=recv_sem,
            device_id=dev,
            device_id_type=MESH,
        ).start()


def take(ref, sem):
    pltpu.make_async_copy(ref, ref, sem).wait()


def features(points, ids, shift, level, w_in, b_in, w_out, inv_scale):
    n = points.shape[0]
    sources = shift.shape[0]
    onehot = (lax.broadcasted_iota(jnp.int32, (sources, n), 0) == ids).astype(jnp.float32)
    eye = lax.broadcasted_iota(jnp.int32, (sources, sources), 0) == lax.broadcasted_iota(
        jnp.int32, (sources, sources), 1
    )
    diag = jnp.where(eye, level, 0.0)
    spread = mm(diag, jnp.ones((sources, 128), jnp.float32))
    noise = mm(onehot, spread, 0, 0)
    shifted = points + mm(onehot, shift, 0, 0)
    hidden = jnp.tanh(mm(shifted, w_in) + b_in)
    scaled = mm(hidden, w_out) * inv_scale
    return scaled, noise


def layout(n, feat):
    groups, per = n // 8, 128 // feat
    return groups, per, -(-(groups + 1) // per)


def pack(scaled, noise):
    n, feat = scaled.shape
    groups, per, tiles = layout(n, feat)
    lane = lax.broadcasted_iota(jnp.int32, (8, feat), 1)
    levels = jnp.zeros((8, feat), jnp.float32)
    for g in range(groups):
        levels = jnp.where(lane == g, noise[8 * g : 8 * g + 8, :feat], levels)
    pieces = [scaled[8 * g : 8 * g + 8] for g in range(groups)] + [levels]
    pieces += [jnp.zeros((8, feat), jnp.float32)] * (per * tiles - groups - 1)
    return jnp.concatenate(
        [jnp.concatenate(pieces[per * t : per * (t + 1)], axis=1) for t in range(tiles)], axis=0
    )


def unpack(packed, n, feat):
    groups, per, tiles = layout(n, feat)
    pieces = []
    for first in range(0, packed.shape[0], 8 * tiles):
        for g in range(groups):
            at, lane = first + 8 * (g // per), feat * (g % per)
            pieces.append(packed[at : at + 8, lane : lane + feat])
    return jnp.concatenate(pieces, axis=0)


def gather_kernel(
    dims, points, ids, shift, level, w_in, b_in, w_out, inv_scale, direction,
    feat_all, dir_col, own, row_feat, col_feat, send_sem, recv_sem,
):
    peers = Peers(*dims)
    rows, cols = dims
    n, feat = points.shape[0], w_out.shape[1]
    high = 8 * layout(n, feat)[2]
    r, c = lax.axis_index("row"), lax.axis_index("col")
    peers.greet()
    scaled, noise = features(
        points[...], ids[...], shift[...], level[...], w_in[...], b_in[...], w_out[...], inv_scale[...]
    )
    mine = pl.ds(pl.multiple_of(peers.me * high, 8), high)
    feat_all[mine, :] = pack(scaled, noise)
    own[...] = jnp.concatenate([scaled, noise[:, feat:]], axis=1)
    block = pl.ds(pl.multiple_of(r * n, 8), n)
    dir_col[block, :] = direction[...]
    peers.meet()
    peers.each(
        lambda t, dev: peers.send(
            feat_all.at[mine], feat_all.at[mine], send_sem.at[0], recv_sem.at[0], dev
        )
    )

    def turn(d, carry):
        dev = {"row": lax.rem(r + d, rows), "col": c}
        peers.send(direction, dir_col.at[block], send_sem.at[1], recv_sem.at[1], dev)
        return carry

    lax.fori_loop(1, rows, turn, 0)
    others = pl.ds(0, (peers.count - 1) * high)
    other_rows = pl.ds(0, (rows - 1) * n)
    take(feat_all.at[others], recv_sem.at[0])
    row_feat[...] = feat_all[pl.ds(pl.multiple_of(r * (cols * high), 8), cols * high), :]
    for q in range(rows):
        col_feat[q * high : (q + 1) * high, :] = feat_all[
            pl.ds(pl.multiple_of((q * cols + c) * high, 8), high), :
        ]
    take(dir_col.at[other_rows], recv_sem.at[1])
    take(feat_all.at[others], send_sem.at[0])
    take(dir_col.at[other_rows], send_sem.at[1])


def local_kernel(
    n, feat_all, dir_col, row_feat, col_feat, own, freq, phase, inverse, capacity, partial, basis_own
):
    feat, rank = freq.shape
    groups, per, tiles = layout(n, feat)
    amp = math.sqrt(2.0 / rank)
    count = feat_all.shape[0] // (8 * tiles)
    diag = lax.broadcasted_iota(jnp.int32, (rank, rank), 0) == lax.broadcasted_iota(
        jnp.int32, (rank, rank), 1
    )
    capacity[...] = jnp.where(diag, 1.0, 0.0)
    view = feat_all[...].reshape(count, tiles, 8, 128)
    levels = view[:, groups // per].reshape(count * 8, 128)
    first = feat * (groups % per)
    for g in range(groups):
        block = view[:, g // per].reshape(count * 8, 128)
        above, below = feat * (g % per), 128 - feat * (g % per + 1)
        wide = [freq[...]]
        if above:
            wide.insert(0, jnp.zeros((above, rank), jnp.float32))
        if below:
            wide.append(jnp.zeros((below, rank), jnp.float32))
        basis = amp * cosine(mm(block, jnp.concatenate(wide, axis=0)) + phase[...])
        capacity[...] += mm(basis, basis / levels[:, first + g : first + g + 1], 0, 0)
    basis_own[...] = amp * cosine(mm(own[...][:, :feat], freq[...]) + phase[...])
    over = unpack(row_feat[...], n, feat)
    under = unpack(col_feat[...], n, feat)
    sq_over = jnp.sum(over * over, axis=1, keepdims=True)
    sq_under = mm(jnp.ones((8, feat), jnp.float32), under * under, 1, 1)[0:1, :]
    distance = sq_over + sq_under - 2.0 * mm(over, under, 1, 1)
    partial[...] = mm(jnp.exp(-0.5 * distance), dir_col[...])
    inverse[...] = invert(capacity[...])


def reduce_kernel(
    dims, owners, own, partial, direction, residual, basis, prior,
    sums, projected, image,
    sums_all, part, slots, blocks, send_sem, recv_sem,
):
    peers = Peers(*dims)
    me, count = peers.me, peers.count
    cols = dims[1]
    n, rhs = direction.shape
    r, c = lax.axis_index("row"), lax.axis_index("col")
    peers.greet()
    noise = own[...][:, 127:128]
    res, d = residual[...], direction[...]
    sres = res / noise
    block = pl.ds(pl.multiple_of(c * n, 8), n)
    blocks[block, :] = partial[block, :]
    peers.meet()

    def turn(k, carry):
        t = lax.rem(c + k, cols)
        peers.send(
            partial.at[pl.ds(pl.multiple_of(t * n, 8), n)],
            blocks.at[block], send_sem.at[3], recv_sem.at[3], {"row": r, "col": t},
        )
        return carry

    lax.fori_loop(1, cols, turn, 0)
    rank = projected.shape[0]
    rq = rank // owners
    proj_res = mm(basis[...], sres, 0, 0).reshape(owners, 1, rq, rhs)
    other_cols = pl.ds(0, (cols - 1) * n)
    take(blocks.at[other_cols], recv_sem.at[3])
    img = jnp.sum(blocks[...].reshape(cols, n, rhs), axis=0) + noise * d
    image[...] = img
    simg = img / noise
    mine = pl.ds(pl.multiple_of(me * 8, 8), 8)
    sums_all[mine, :] = jnp.concatenate(
        [
            jnp.sum(d * img, axis=0, keepdims=True),
            jnp.sum(res * sres, axis=0, keepdims=True),
            jnp.sum(res * simg, axis=0, keepdims=True),
            jnp.sum(img * simg, axis=0, keepdims=True),
            jnp.zeros((4, rhs), jnp.float32),
        ],
        axis=0,
    )
    proj_img = mm(basis[...], simg, 0, 0).reshape(owners, 1, rq, rhs)
    part[...] = jnp.concatenate([proj_res, proj_img], axis=1).reshape(2 * rank, rhs)
    slot = pl.ds(pl.multiple_of(me * (2 * rq), 8), 2 * rq)

    def scatter(t, dev):
        def go():
            peers.send(
                part.at[pl.ds(pl.multiple_of(t * (2 * rq), 8), 2 * rq)],
                slots.at[slot], send_sem.at[1], recv_sem.at[1], dev,
            )

        peers.send(sums_all.at[mine], sums_all.at[mine], send_sem.at[0], recv_sem.at[0], dev)
        if owners < count:
            pl.when(t < owners)(go)
        else:
            go()

    peers.each(scatter)
    other_sums = pl.ds(0, (count - 1) * 8)
    take(sums_all.at[other_sums], recv_sem.at[0])
    totals = jnp.sum(sums_all[...].reshape(count, 8, rhs), axis=0)
    sums[...] = totals
    alpha = prior[...] / totals[0:1, :]

    def owner():
        result = pl.ds(pl.multiple_of(me * rq, 8), rq)
        slots[slot, :] = part[slot, :]
        take(slots.at[pl.ds(0, (count - 1) * 2 * rq)], recv_sem.at[1])
        both = jnp.sum(slots[...].reshape(count, 2 * rq, rhs), axis=0)
        projected[result, :] = both[:rq] - alpha * both[rq:]
        if owners > 1:
            take(part.at[pl.ds(0, (owners - 1) * 2 * rq)], send_sem.at[1])
        peers.each(
            lambda t, dev: peers.send(
                projected.at[result], projected.at[result], send_sem.at[2], recv_sem.at[2], dev
            )
        )
        if owners > 1:
            take(projected.at[pl.ds(0, (owners - 1) * rq)], recv_sem.at[2])
        take(slots.at[pl.ds(0, (count - 1) * rq)], send_sem.at[2])

    def guest():
        take(projected, recv_sem.at[2])
        take(part, send_sem.at[1])

    if owners < count:
        pl.when(me < owners)(owner)
        pl.when(me >= owners)(guest)
    else:
        owner()
    take(sums_all.at[other_sums], send_sem.at[0])
    take(blocks.at[other_cols], send_sem.at[3])


def final_kernel(
    inverse, capacity, projected, sums, own, image, direction, residual, sol, basis, prior,
    new_sol, new_res, new_dir, new_prod,
):
    proj, tot = projected[...], sums[...]
    alpha = prior[...] / tot[0:1, :]
    coeffs = mm(inverse[...], proj)
    coeffs = coeffs + mm(inverse[...], proj - mm(capacity[...], coeffs))
    noise = own[...][:, 127:128]
    d = direction[...]
    nres = residual[...] - alpha * image[...]
    norm = tot[1:2, :] - 2.0 * alpha * tot[2:3, :] + alpha * alpha * tot[3:4, :]
    prod = norm - jnp.sum(proj * coeffs, axis=0, keepdims=True)
    precond = (nres - mm(basis[...], coeffs)) / noise
    new_sol[...] = sol[...] + alpha * d
    new_res[...] = nres
    new_dir[...] = precond + prod / prior[...] * d
    new_prod[...] = prod


def per_device(
    dims, points, source_ids, source_shift, noise_level, weight_in, bias_in, weight_out,
    inverse_scale, frequency, phase_shift, solution, residual, direction, prior_product,
):
    count = dims[0] * dims[1]
    n, rhs = direction.shape
    feat, rank = frequency.shape
    f32 = jnp.float32
    sds = jax.ShapeDtypeStruct
    row = lambda v: v.reshape(1, -1)
    dma = pltpu.SemaphoreType.DMA
    prior = row(prior_product)
    high = 8 * layout(n, feat)[2]
    feat_all, dir_col, own, row_feat, col_feat = pl.pallas_call(
        functools.partial(gather_kernel, dims),
        out_shape=(
            sds((count * high, 128), f32), sds((dims[0] * n, rhs), f32), sds((n, 128), f32),
            sds((dims[1] * high, 128), f32), sds((dims[0] * high, 128), f32),
        ),
        in_specs=[VMEM] * 9,
        out_specs=(VMEM,) * 5,
        scratch_shapes=[dma((2,)), dma((2,))],
        compiler_params=pltpu.CompilerParams(collective_id=0, has_side_effects=True),
        name="gather",
    )(
        points, row(source_ids), source_shift, row(noise_level), weight_in, row(bias_in),
        weight_out, row(inverse_scale), direction,
    )
    phase = row(phase_shift)
    square = sds((rank, rank), f32)
    inverse, capacity, partial, basis = pl.pallas_call(
        functools.partial(local_kernel, n),
        out_shape=(square, square, sds((dims[1] * n, rhs), f32), sds((n, rank), f32)),
        in_specs=[VMEM] * 7,
        out_specs=(VMEM,) * 4,
        name="local",
    )(feat_all, dir_col, row_feat, col_feat, own, frequency, phase)
    owners = min(count, rank // 8)
    sums, projected, image = pl.pallas_call(
        functools.partial(reduce_kernel, dims, owners),
        out_shape=(sds((8, rhs), f32), sds((rank, rhs), f32), sds((n, rhs), f32)),
        in_specs=[VMEM] * 6,
        out_specs=(VMEM,) * 3,
        scratch_shapes=[
            pltpu.VMEM((8 * count, rhs), f32),
            pltpu.VMEM((2 * rank, rhs), f32),
            pltpu.VMEM((count * (2 * rank // owners), rhs), f32),
            pltpu.VMEM((dims[1] * n, rhs), f32),
            dma((4,)),
            dma((4,)),
        ],
        compiler_params=pltpu.CompilerParams(collective_id=1, has_side_effects=True),
        name="reduce",
    )(own, partial, direction, residual, basis, prior)
    block = sds((n, rhs), f32)
    new_sol, new_res, new_dir, new_prod = pl.pallas_call(
        final_kernel,
        out_shape=(block, block, block, sds((1, rhs), f32)),
        in_specs=[VMEM] * 11,
        out_specs=(VMEM,) * 4,
        name="final",
    )(inverse, capacity, projected, sums, own, image, direction, residual, solution, basis, prior)
    return new_sol, new_res, new_dir, new_prod.reshape(rhs)


def solution(mesh):
    dims = (mesh.shape["row"], mesh.shape["col"])
    rows = P(("row", "col"), None)
    in_specs = (
        rows, P(("row", "col")), P(), P(), P(), P(), P(), P(), P(), P(), rows, rows, rows, P(),
    )
    return jax.shard_map(
        functools.partial(per_device, dims),
        mesh=mesh,
        in_specs=in_specs,
        out_specs=(rows, rows, rows, P()),
        check_vma=False,
    )
```

profile of v0, /device:TPU:0, one launch (start us, length us, event | category | flops | bytes accessed | tf_op | source)
XLA Modules:
  0.0 64.4 jit_solution(17775701794745874227)
XLA Ops:
  0.6 1.5 %copy.18.w_out = f32[256,32]{1,0:T(8,128)} copy(f32[256,32]{0,1:T(8,128)} %param.20) | data formatting | bytes 65536 | tf_op args[6]
  2.1 15.8 %gather.1 = (f32[512,128]{1,0:T(8,128)}, f32[160,128]{1,0:T(8,128)}, f32[40,128]{1,0:T(8,128)}, f32[128,128]{1,0:T(8,128)}, f32[64,128]{1,0:T(8,128)}) custom-call(f32[40,128]{1,0:T(8,128)} %points.1, s32[1,40]{1,0:T(1,128)} %bitcast.11, f32[64,128]{1,0:T(8,128)} %shift.1, f32[1,64]{1,0:T(1,128)} %bitcast.12, f32[128,256]{1,0:T(8,128)} %w_in.1, ...), custom_call_target="tpu_custom_call" | custom-call | tf_op jit(solution)/shard_map/gather/pallas_call | solution.py:417
  17.9 16.6 %local.1 = (f32[256,256]{1,0:T(8,128)}, f32[256,256]{1,0:T(8,128)}, f32[320,128]{1,0:T(8,128)}, f32[40,256]{1,0:T(8,128)}) custom-call(f32[512,128]{1,0:T(8,128)} %get-tuple-element.20.feat_all, f32[160,128]{1,0:T(8,128)} %get-tuple-element.21.dir_col, f32[128,128]{1,0:T(8,128)} %get-tuple-element.22.row_feat, f32[64,128]{1,0:T(8,128)} %get-tuple-element.23.col_feat, ...), custom_call_target="tpu_custom_call" | custom-call | tf_op jit(solution)/shard_map/local/pallas_call | solution.py:434
  34.5 26.5 %reduce.1 = (f32[8,128]{1,0:T(8,128)}, f32[256,128]{1,0:T(8,128)}, f32[40,128]{1,0:T(8,128)}) custom-call(f32[40,128]{1,0:T(8,128)} %get-tuple-element.24.own, f32[320,128]{1,0:T(8,128)} %get-tuple-element.27.partial, f32[40,128]{1,0:T(8,128)} %direction.5, f32[40,128]{1,0:T(8,128)} %residual.3, f32[40,256]{1,0:T(8,128)} %get-tuple-element.28.basis, ...), custom_call_target="tpu_custom_call" | custom-call | tf_op jit(solution)/shard_map/reduce/pallas_call | solution.py:442
  61.0 3.3 %final.1 = (f32[40,128]{1,0:T(8,128)}, f32[40,128]{1,0:T(8,128)}, f32[40,128]{1,0:T(8,128)}, f32[1,128]{1,0:T(1,128)}) custom-call(f32[256,256]{1,0:T(8,128)} %get-tuple-element.25.inverse, f32[256,256]{1,0:T(8,128)} %get-tuple-element.26.capacity, f32[256,128]{1,0:T(8,128)} %get-tuple-element.29.projected, f32[8,128]{1,0:T(8,128)} %get-tuple-element.30.sums, ...), custom_call_target="tpu_custom_call" | custom-call | tf_op jit(solution)/shard_map/final/pallas_call | solution.py:459
where the time goes:
time: 64.6 us; the launch traced here: 64.4 us
  Pallas kernels  62.2 us (96%)
  local copies, waits for them, and re-layouts  1.5 us (2%)
  between operations  0.65 us (1%)
    pallas_call x1, Pallas kernels, per_device(): pl.pallas_call(functools.partial(reduce_kernel, dims, owners), out_shape=...  26.5 us
    pallas_call x1, Pallas kernels, per_device(): pl.pallas_call(functools.partial(local_kernel, n), out_shape=(square, squ...  16.6 us
    pallas_call x1, Pallas kernels, per_device(): pl.pallas_call(functools.partial(gather_kernel, dims), out_shape=(sds((co...  15.8 us
    pallas_call x1, Pallas kernels, per_device(): pl.pallas_call(final_kernel, out_shape=(block, block, block, sds((1, rhs)...  3.34 us
    unnamed x1, local copies, waits for them, and re-layouts  1.5 us

commit v1 on v0

--- a/solution.py
+++ b/solution.py
@@ -7,7 +7,6 @@
 from jax.experimental import pallas as pl
 from jax.experimental.pallas import tpu as pltpu
 from jax.sharding import PartitionSpec as P
-
 HIGH = lax.Precision.HIGHEST
 MESH = pl.DeviceIdType.MESH
 VMEM = pl.BlockSpec(memory_space=pltpu.VMEM)
@@ -170,7 +169,7 @@
     noise = mm(onehot, spread, 0, 0)
     shifted = points + mm(onehot, shift, 0, 0)
     hidden = jnp.tanh(mm(shifted, w_in) + b_in)
-    scaled = mm(hidden, w_out) * inv_scale
+    scaled = mm(hidden, w_out, 1, 1) * inv_scale
     return scaled, noise
 
 
@@ -209,7 +208,7 @@
 ):
     peers = Peers(*dims)
     rows, cols = dims
-    n, feat = points.shape[0], w_out.shape[1]
+    n, feat = points.shape[0], w_out.shape[0]
     high = 8 * layout(n, feat)[2]
     r, c = lax.axis_index("row"), lax.axis_index("col")
     peers.greet()
@@ -427,7 +426,7 @@
         name="gather",
     )(
         points, row(source_ids), source_shift, row(noise_level), weight_in, row(bias_in),
-        weight_out, row(inverse_scale), direction,
+        weight_out.T, row(inverse_scale), direction,
     )
     phase = row(phase_shift)
     square = sds((rank, rank), f32)
@@ -466,6 +465,346 @@
     return new_sol, new_res, new_dir, new_prod.reshape(rhs)
 
 
+BF16 = jnp.bfloat16
+
+
+def dot(a, b, ca=1, cb=0):
+    return lax.dot_general(a, b, (((ca,), (cb,)), ((), ())), preferred_element_type=jnp.float32)
+
+
+def split(x):
+    high = x.astype(BF16)
+    rest = x - high.astype(jnp.float32)
+    mid = rest.astype(BF16)
+    low = (rest - mid.astype(jnp.float32)).astype(BF16)
+    return high, mid, low
+
+
+def rows_of(x):
+    parts = [p.astype(jnp.float32) for p in split(x)]
+    fill = -3 * x.shape[0] % 16
+    if fill:
+        parts.append(jnp.zeros((fill, x.shape[1]), jnp.float32))
+    return jnp.concatenate(parts, axis=0).astype(BF16)
+
+
+def fold(acc, q):
+    return acc[0:q] + acc[q : 2 * q] + acc[2 * q : 3 * q]
+
+
+def iota(shape, dim):
+    return lax.broadcasted_iota(jnp.int32, shape, dim)
+
+
+class Plan:
+    def __init__(self, dims, n, rhs, feat):
+        self.count = dims[0] * dims[1]
+        self.n, self.rhs, self.feat = n, rhs, feat
+        self.q = rhs // self.count
+        self.per = 128 // n
+        self.windows = -(-self.count // self.per)
+        self.wide = 128 * self.windows
+        self.groups = n // 8
+        self.pieces = 128 // feat - 1
+        self.tiles = -(-self.groups // self.pieces)
+
+    def fits(self):
+        return (
+            self.rhs == 128
+            and self.rhs % self.count == 0
+            and self.q % 4 == 0
+            and 2 * self.n + 2 <= 128
+            and self.n % 8 == 0
+            and self.groups <= 8
+            and self.feat % 16 == 0
+            and self.feat <= 32
+            and self.wide <= 2048
+        )
+
+
+def cosine_turns(u):
+    r = u - jnp.round(u)
+    z = r * r
+    p = SIN[-1]
+    for c in SIN[-2::-1]:
+        p = p * z + c
+    s = p * r
+    return 1.0 - 2.0 * (s * s)
+
+
+SIN = tuple((-1.0) ** i * math.pi ** (2 * i + 1) / math.factorial(2 * i + 1) for i in range(8))
+
+
+def pack_tiles(plan, scaled, noise):
+    feat = plan.feat
+    lane = iota((8, feat), 1)
+    levels = jnp.zeros((8, feat), jnp.float32)
+    for g in range(plan.groups):
+        levels = jnp.where(lane == g, noise[8 * g : 8 * g + 8, :feat], levels)
+    tiles = []
+    for t in range(plan.tiles):
+        row = []
+        for j in range(plan.pieces):
+            g = t * plan.pieces + j
+            row.append(
+                scaled[8 * g : 8 * g + 8] if g < plan.groups else jnp.zeros((8, feat), jnp.float32)
+            )
+        tiles.append(jnp.concatenate(row + [levels], axis=1))
+    return tiles
+
+
+def unpack_tiles(plan, feat_all):
+    n, feat, per = plan.n, plan.feat, plan.per
+    group = lax.rem(iota((8, 128), 1), n) // 8
+    place = lax.rem(group, plan.pieces)[0:1]
+    zero = jnp.zeros((8, 128), jnp.float32)
+    features, levels = [], []
+    for w in range(plan.windows):
+        rows = []
+        for k in range(per):
+            s = w * per + k
+            for g in range(plan.groups):
+                rows.append(feat_all[s, g // plan.pieces] if s < plan.count else zero)
+        rows += [zero] * (16 - len(rows))
+        turned = jnp.concatenate(rows, axis=0).T
+        out = turned[(plan.pieces - 1) * feat : plan.pieces * feat]
+        for j in range(plan.pieces - 1):
+            out = jnp.where(place == j, turned[j * feat : (j + 1) * feat], out)
+        features.append(out)
+        base = plan.pieces * feat
+        level = jnp.where(iota((8, 128), 0) == group, turned[base : base + 8], 0.0)
+        levels.append(jnp.sum(level, axis=0, keepdims=True))
+    return jnp.concatenate(features, axis=1), jnp.concatenate(levels, axis=1)
+
+
+def live_lanes(plan):
+    lane = iota((1, plan.wide), 1)
+    inside = lax.rem(lane, 128)
+    source = (lane // 128) * plan.per + inside // plan.n
+    return (inside < plan.per * plan.n) & (source < plan.count)
+
+
+def between(lane, start, n):
+    first = start % 128
+    last = first + n
+    if last <= 128:
+        return (lane >= first) & (lane < last)
+    return (lane >= first) | (lane < last - 128)
+
+
+def main_kernel(
+    dims, points, ids, shift, level, w_in, b_in, w_out, inv_scale, freq, phase,
+    residual, direction, prior,
+    out_all,
+    feat_all, turned, slabs, outs, right, left, capacity, inverse, basis, send_sem, recv_sem,
+):
+    peers = Peers(*dims)
+    me, count = peers.me, peers.count
+    n, rhs = direction.shape
+    feat, rank = freq.shape
+    plan = Plan(dims, n, rhs, feat)
+    q, per, wide, windows = plan.q, plan.per, plan.wide, plan.windows
+    f32 = jnp.float32
+    peers.greet()
+    scaled, noise = features(
+        points[...], ids[...], shift[...], level[...], w_in[...], b_in[...], w_out[...], inv_scale[...]
+    )
+    for t, tile in enumerate(pack_tiles(plan, scaled, noise)):
+        feat_all[me, t] = tile
+    peers.meet()
+    peers.each(
+        lambda t, dev: peers.send(
+            feat_all.at[me], feat_all.at[me], send_sem.at[0], recv_sem.at[0], dev
+        )
+    )
+    stacked = jnp.concatenate(
+        [direction[...], residual[...], prior[...], jnp.zeros((127 - 2 * n, rhs), f32)], axis=0
+    )
+    spun = pltpu.roll(stacked.T, n * lax.rem(me, per), 1)
+    for t in range(count):
+        turned[t] = spun[t * q : (t + 1) * q]
+    slabs[me] = turned[me]
+    peers.each(
+        lambda t, dev: peers.send(
+            turned.at[t], slabs.at[me], send_sem.at[1], recv_sem.at[1], dev
+        )
+    )
+    turn = 1.0 / (2.0 * math.pi)
+    both = jnp.concatenate([freq[...], phase[...], jnp.zeros((127 - feat, rank), f32)], axis=0) * turn
+    fp = both.T
+    fh, fm, fl = [p.astype(f32) for p in split(fp)]
+    fills = 256 - 6 * feat - 3
+    spectral = jnp.concatenate(
+        [fh[:, :feat], fh[:, :feat], fh[:, :feat], fm[:, :feat], fm[:, :feat], fl[:, :feat]]
+        + [p[:, feat : feat + 1] for p in (fh, fm, fl)]
+        + [jnp.zeros((rank, fills), f32)],
+        axis=1,
+    ).astype(BF16)
+    lane = iota((1, 128), 1)
+    live = live_lanes(plan)
+
+    take(feat_all.at[pl.ds(0, count - 1)], recv_sem.at[0])
+    ft, levels = unpack_tiles(plan, feat_all)
+    levels = jnp.where(live, levels, 1.0)
+    rsn = jnp.where(live, lax.rsqrt(levels), 0.0)
+    h, m, l = split(ft)
+    scale2 = math.log2(math.e)
+    ft2 = ft * scale2
+    h2, m2, l2 = split(ft2)
+    sq = -0.5 * jnp.sum(ft2 * ft, axis=0, keepdims=True)
+    sqs = [p.astype(f32) for p in split(sq)]
+    ones = jnp.ones((3, wide), f32)
+    tail = 256 - 6 * feat
+    rest = jnp.zeros((tail - 6, wide), f32)
+    right[...] = jnp.concatenate(
+        [h, m, l, h, m, h, jnp.concatenate([ones] + sqs + [rest], axis=0).astype(BF16)], axis=0
+    )
+    low = jnp.concatenate(
+        [h2, h2, h2, m2, m2, l2, jnp.concatenate(sqs + [ones, rest], axis=0).astype(BF16)], axis=0
+    )
+    left[...] = low.T
+    amp = math.sqrt(2.0 / rank)
+    u = dot(spectral, right[...])
+    c = cosine_turns(u) * (amp * rsn)
+    ch, cm, cl = split(c)
+    basis[0] = ch
+    basis[1] = cm
+    basis[2] = cl
+    diag = iota((rank, rank), 0) == iota((rank, rank), 1)
+    capacity[...] = (
+        jnp.where(diag, 1.0, 0.0)
+        + dot(ch, ch, 1, 1) + (dot(ch, cm, 1, 1) + dot(cm, ch, 1, 1))
+        + (dot(cm, cm, 1, 1) + dot(ch, cl, 1, 1) + dot(cl, ch, 1, 1))
+    )
+    inverse[...] = invert(capacity[...])
+
+    take(slabs.at[pl.ds(0, count - 1)], recv_sem.at[1])
+    zero = jnp.zeros((q, 128), f32)
+    dirs, ress = [], []
+    for w in range(windows):
+        own = [slabs[w * per + k] if w * per + k < count else zero for k in range(per)]
+        d, r = zero, zero
+        for k in range(per):
+            d = jnp.where(between(lane, k * n, n), own[k], d)
+            r = jnp.where(between(lane, (k + 1) * n, n), own[k], r)
+        dirs.append(d)
+        ress.append(pltpu.roll(r, 128 - n, 1))
+    d = jnp.concatenate(dirs, axis=1)
+    r = jnp.concatenate(ress, axis=1)
+    mine = pltpu.roll(slabs[me], 128 - n * lax.rem(me, per), 1)
+    own_prior = mine[:, 2 * n : 2 * n + 1]
+    d3 = rows_of(d)
+    acc = jnp.zeros((d3.shape[0], wide), f32)
+    for w in range(windows):
+        e = dot(left[w * 128 : (w + 1) * 128, :], right[...])
+        k = jnp.exp2(e)
+        kh = k.astype(BF16)
+        kl = (k - kh.astype(f32)).astype(BF16)
+        part = d3[:, w * 128 : (w + 1) * 128]
+        acc = acc + (dot(part, kh) + dot(part, kl))
+    img = fold(acc, q) + levels * d
+    alpha = own_prior / jnp.sum(d * img, axis=1, keepdims=True)
+    nres = r - alpha * img
+    y = nres * rsn
+    y3 = rows_of(y)
+    proj = fold(
+        dot(y3, basis[0], 1, 1) + dot(y3, basis[1], 1, 1) + dot(y3, basis[2], 1, 1), q
+    )
+    coeffs = mm(proj, inverse[...])
+    coeffs = coeffs + mm(proj - mm(coeffs, capacity[...]), inverse[...])
+    c3 = rows_of(coeffs)
+    back = fold(dot(c3, basis[0]) + dot(c3, basis[1]) + dot(c3, basis[2]), q)
+    precond = (y - back) * rsn
+    prod = jnp.sum(nres * precond, axis=1, keepdims=True)
+    ndir = precond + prod / own_prior * d
+    for w in range(windows):
+        part = nres[:, w * 128 : (w + 1) * 128]
+        side = pltpu.roll(ndir[:, w * 128 : (w + 1) * 128], n, 1)
+        for k in range(per):
+            t = w * per + k
+            if t < count:
+                slab = jnp.where(lane == (k * n + 2 * n) % 128, alpha, prod)
+                slab = jnp.where(between(lane, (k + 1) * n, n), side, slab)
+                outs[t] = jnp.where(between(lane, k * n, n), part, slab)
+    out_all[me] = outs[me]
+    peers.each(
+        lambda t, dev: peers.send(outs.at[t], out_all.at[me], send_sem.at[2], recv_sem.at[2], dev)
+    )
+    others = pl.ds(0, count - 1)
+    take(out_all.at[others], recv_sem.at[2])
+    take(feat_all.at[others], send_sem.at[0])
+    take(slabs.at[others], send_sem.at[1])
+    take(out_all.at[others], send_sem.at[2])
+
+
+def finish_kernel(dims, got, direction, sol, new_sol, new_res, new_dir, new_prod):
+    me = lax.axis_index("row") * dims[1] + lax.axis_index("col")
+    n = direction.shape[0]
+    per = 128 // n
+    back = lax.rem(128 - n * lax.rem(me, per), 128)
+    x = pltpu.roll(got[...], back, 1).T
+    new_res[...] = x[0:n]
+    new_dir[...] = x[n : 2 * n]
+    new_sol[...] = sol[...] + x[2 * n : 2 * n + 1] * direction[...]
+    new_prod[...] = x[2 * n + 1 : 2 * n + 2]
+
+
+def per_device_columns(
+    dims, points, source_ids, source_shift, noise_level, weight_in, bias_in, weight_out,
+    inverse_scale, frequency, phase_shift, solution, residual, direction, prior_product,
+):
+    n, rhs = direction.shape
+    feat, rank = frequency.shape
+    plan = Plan(dims, n, rhs, feat)
+    count, q, wide = plan.count, plan.q, plan.wide
+    f32 = jnp.float32
+    sds = jax.ShapeDtypeStruct
+    row = lambda v: v.reshape(1, -1)
+    dma = pltpu.SemaphoreType.DMA
+    got = pl.pallas_call(
+        functools.partial(main_kernel, dims),
+        out_shape=sds((count, q, 128), f32),
+        in_specs=[VMEM] * 13,
+        out_specs=VMEM,
+        scratch_shapes=[
+            pltpu.VMEM((count, plan.tiles, 8, 128), f32),
+            pltpu.VMEM((count, q, 128), f32),
+            pltpu.VMEM((count, q, 128), f32),
+            pltpu.VMEM((count, q, 128), f32),
+            pltpu.VMEM((256, wide), BF16),
+            pltpu.VMEM((wide, 256), BF16),
+            pltpu.VMEM((rank, rank), f32),
+            pltpu.VMEM((rank, rank), f32),
+            pltpu.VMEM((3, rank, wide), BF16),
+            dma((3,)),
+            dma((3,)),
+        ],
+        compiler_params=pltpu.CompilerParams(collective_id=0, has_side_effects=True),
+        name="columns",
+    )(
+        points, row(source_ids), source_shift, row(noise_level), weight_in, row(bias_in),
+        weight_out.T, row(inverse_scale), frequency, row(phase_shift), residual, direction,
+        row(prior_product),
+    )
+    block = sds((n, rhs), f32)
+    new_sol, new_res, new_dir, new_prod = pl.pallas_call(
+        functools.partial(finish_kernel, dims),
+        out_shape=(block, block, block, sds((1, rhs), f32)),
+        in_specs=[VMEM] * 3,
+        out_specs=(VMEM,) * 4,
+        name="finish",
+    )(got.reshape(rhs, 128), direction, solution)
+    return new_sol, new_res, new_dir, new_prod.reshape(rhs)
+
+
+def dispatch(dims, *args):
+    n, rhs = args[12].shape
+    feat = args[8].shape[0]
+    if Plan(dims, n, rhs, feat).fits():
+        return per_device_columns(dims, *args)
+    return per_device(dims, *args)
+
+
 def solution(mesh):
     dims = (mesh.shape["row"], mesh.shape["col"])
     rows = P(("row", "col"), None)
@@ -473,7 +812,7 @@
         rows, P(("row", "col")), P(), P(), P(), P(), P(), P(), P(), P(), rows, rows, rows, P(),
     )
     return jax.shard_map(
-        functools.partial(per_device, dims),
+        functools.partial(dispatch, dims),
         mesh=mesh,
         in_specs=in_specs,
         out_specs=(rows, rows, rows, P()),

time: 64.6 us -> 46 us (0.71)
  Pallas kernels: 62.2 us -> 45.2 us
  local copies, waits for them, and re-layouts: 1.5 us -> 0 us
    pallas_call x4 -> x2, Pallas kernels: 62.2 us -> 45.2 us  [the longest x1 43.5 us: per_device_columns(): pl.pallas_call(functools.partial(main_kernel, dims), out_shape=sds((count...]
    unnamed x1 -> x0, local copies, waits for them, and re-layouts: 1.5 us -> none
where the time goes in v1:
time: 46 us; the launch traced here: 45.8 us
  Pallas kernels  45.2 us (98%)
  between operations  0.64 us (1%)
    pallas_call x1, Pallas kernels, per_device_columns(): pl.pallas_call(functools.partial(main_kernel, dims), out_shape=sds((count...  43.5 us
    pallas_call x1, Pallas kernels, per_device_columns(): pl.pallas_call(functools.partial(finish_kernel, dims), out_shape=(block,...  1.64 us

profile of v1, /device:TPU:0, one launch (start us, length us, event | category | flops | bytes accessed | tf_op | source)
XLA Modules:
  0.0 45.8 jit_solution(15456996729883823687)
XLA Ops:
  0.6 43.5 %columns.1 = f32[32,4,128]{2,1,0:T(4,128)} custom-call(f32[40,128]{1,0:T(8,128)} %points.1, s32[1,40]{1,0:T(1,128)} %bitcast.13, f32[64,128]{1,0:T(8,128)} %shift.1, f32[1,64]{1,0:T(1,128)} %bitcast.14, f32[128,256]{1,0:T(8,128)} %w_in.1, f32[1,256]{1,0:T(1,128)} %bitcast.11, f32[32,256]{1,0:T(8,128)} %bitcast.10, f32[1,32]{1,0:T(1,128)} %bitcast.15, ...), custom_call_target="tpu_custom_call" | custom-call | tf_op jit(solution)/shard_map/columns/pallas_call | solution.py:764
  44.2 1.6 %finish.1 = (f32[40,128]{1,0:T(8,128)}, f32[40,128]{1,0:T(8,128)}, f32[40,128]{1,0:T(8,128)}, f32[1,128]{1,0:T(1,128)}) custom-call(f32[128,128]{1,0:T(8,128)} %bitcast.9, f32[40,128]{1,0:T(8,128)} %direction.3, f32[40,128]{1,0:T(8,128)} %sol.1), custom_call_target="tpu_custom_call" | custom-call | tf_op jit(solution)/shard_map/finish/pallas_call | solution.py:790

commit v2 on v1

--- a/solution.py
+++ b/solution.py
@@ -496,24 +496,140 @@
     return lax.broadcasted_iota(jnp.int32, shape, dim)
 
 
+def pivot_inverse(at):
+    a00, a01, a11 = at(0, 0), at(0, 1), at(1, 1)
+    b00, b01, b10, b11 = at(0, 2), at(0, 3), at(1, 2), at(1, 3)
+    d00, d01, d11 = at(2, 2), at(2, 3), at(3, 3)
+    inv = 1.0 / (a00 * a11 - a01 * a01)
+    e00, e01, e11 = a11 * inv, -a01 * inv, a00 * inv
+    f00, f01 = e00 * b00 + e01 * b10, e00 * b01 + e01 * b11
+    f10, f11 = e01 * b00 + e11 * b10, e01 * b01 + e11 * b11
+    s00 = d00 - (b00 * f00 + b10 * f10)
+    s01 = d01 - (b00 * f01 + b10 * f11)
+    s11 = d11 - (b01 * f01 + b11 * f11)
+    inv = 1.0 / (s00 * s11 - s01 * s01)
+    t00, t01, t11 = s11 * inv, -s01 * inv, s00 * inv
+    g00, g01 = f00 * t00 + f01 * t01, f00 * t01 + f01 * t11
+    g10, g11 = f10 * t00 + f11 * t01, f10 * t01 + f11 * t11
+    p00 = e00 + g00 * f00 + g01 * f01
+    p01 = e01 + g00 * f10 + g01 * f11
+    p11 = e11 + g10 * f10 + g11 * f11
+    return (
+        (p00, p01, -g00, -g01),
+        (p01, p11, -g10, -g11),
+        (-g00, -g10, t00, t01),
+        (-g01, -g11, t01, t11),
+    )
+
+
+def column(m, at):
+    lane = lax.broadcasted_iota(jnp.int32, m.shape, 1)
+    return jnp.broadcast_to(jnp.sum(jnp.where(lane == at, m, 0.0), axis=1, keepdims=True), m.shape)
+
+
+def sweep(rows, first):
+    size, wide = rows.shape
+    groups, tiles = size // 8, wide // 128
+    full = (8, 128)
+    m = [[rows[8 * g : 8 * g + 8, t * 128 : (t + 1) * 128] for t in range(tiles)] for g in range(groups)]
+    lane = lax.broadcasted_iota(jnp.int32, full, 1)
+    sub = lax.broadcasted_iota(jnp.int32, full, 0)
+
+    def line(x, i):
+        return jnp.broadcast_to(x[i : i + 1, :], full)
+
+    def columns(row, k):
+        home, at0 = divmod(first + k, 128)
+        return [column(row[home], at0 + j) for j in range(4)]
+
+    near = columns(m[0], 0)
+    for k in range(0, size, 4):
+        group, off = divmod(k, 8)
+        home, at0 = divmod(first + k, 128)
+        cols = [columns(m[g], k) for g in range(groups)]
+        pivots = pivot_inverse(lambda i, j: line(near[j], off + i))
+        if k + 4 < size:
+            after = (k + 4) // 8
+            ahead = columns(m[after], k + 4)
+            other = ahead if after == group else columns(m[group], k + 4)
+            past = [[line(other[j], off + l) for l in range(4)] for j in range(4)]
+            c = cols[after]
+            gain = [
+                (c[0] * pivots[0][l] + c[1] * pivots[1][l]) + (c[2] * pivots[2][l] + c[3] * pivots[3][l])
+                for l in range(4)
+            ]
+            near = [
+                ahead[j]
+                - ((gain[0] * past[j][0] + gain[1] * past[j][1]) + (gain[2] * past[j][2] + gain[3] * past[j][3]))
+                for j in range(4)
+            ]
+        inside = (lane >= at0) & (lane < at0 + 4)
+        out = [[None] * tiles for _ in range(groups)]
+        for t in range(tiles):
+            own = [line(m[group][t], off + l) for l in range(4)]
+            if t == home:
+                own = [
+                    jnp.where(lane == at0 + l, 1.0, jnp.where(inside, 0.0, own[l])) for l in range(4)
+                ]
+            scaled = [(p[0] * own[0] + p[1] * own[1]) + (p[2] * own[2] + p[3] * own[3]) for p in pivots]
+            for g in range(groups):
+                base = jnp.where(inside, 0.0, m[g][t]) if t == home else m[g][t]
+                c = cols[g]
+                x = base - (
+                    (c[0] * scaled[0] + c[1] * scaled[1]) + (c[2] * scaled[2] + c[3] * scaled[3])
+                )
+                if g == group:
+                    for l in range(4):
+                        x = jnp.where(sub == off + l, scaled[l], x)
+                out[g][t] = x
+        m = out
+    return jnp.concatenate([jnp.concatenate(r, axis=1) for r in m], axis=0)
+
+
+def exact(a, b):
+    ah, am, al = split(a)
+    bh, bm, bl = split(b)
+    return dot(ah, bh) + (dot(ah, bm) + dot(am, bh)) + (dot(am, bm) + dot(ah, bl) + dot(al, bh))
+
+
+def invert_panels(a):
+    size = a.shape[0]
+    step = min(128, size)
+    lane = iota((1, size), 1)
+    for k in range(0, size, step):
+        rows = sweep(a[k : k + step], k)
+        pieces = [(k, rows)]
+        for lo, hi in ((0, k), (k + step, size)):
+            if hi > lo:
+                part = a[lo:hi]
+                base = jnp.where((lane >= k) & (lane < k + step), 0.0, part)
+                pieces.append((lo, base - exact(part[:, k : k + step], rows)))
+        pieces.sort(key=lambda v: v[0])
+        a = jnp.concatenate([p for _, p in pieces], axis=0) if len(pieces) > 1 else rows
+    return a
+
+
 class Plan:
     def __init__(self, dims, n, rhs, feat):
         self.count = dims[0] * dims[1]
+        self.pairs = self.count // 2
         self.n, self.rhs, self.feat = n, rhs, feat
-        self.q = rhs // self.count
+        self.q = rhs // self.pairs
         self.per = 128 // n
         self.windows = -(-self.count // self.per)
         self.wide = 128 * self.windows
         self.groups = n // 8
         self.pieces = 128 // feat - 1
         self.tiles = -(-self.groups // self.pieces)
+        self.even = dims[0] % 2 == 0
 
     def fits(self):
         return (
-            self.rhs == 128
-            and self.rhs % self.count == 0
-            and self.q % 4 == 0
-            and 2 * self.n + 2 <= 128
+            self.even
+            and self.rhs == 128
+            and self.q == 8
+            and 2 * self.n + 1 <= 128
+            and self.per * self.n < 128
             and self.n % 8 == 0
             and self.groups <= 8
             and self.feat % 16 == 0
@@ -532,7 +648,7 @@
     return 1.0 - 2.0 * (s * s)
 
 
-SIN = tuple((-1.0) ** i * math.pi ** (2 * i + 1) / math.factorial(2 * i + 1) for i in range(8))
+SIN = tuple((-1.0) ** i * math.pi ** (2 * i + 1) / math.factorial(2 * i + 1) for i in range(7))
 
 
 def pack_tiles(plan, scaled, noise):
@@ -564,7 +680,7 @@
         for k in range(per):
             s = w * per + k
             for g in range(plan.groups):
-                rows.append(feat_all[s, g // plan.pieces] if s < plan.count else zero)
+                rows.append(feat_all[s // plan.pairs, s % plan.pairs, g // plan.pieces] if s < plan.count else zero)
         rows += [zero] * (16 - len(rows))
         turned = jnp.concatenate(rows, axis=0).T
         out = turned[(plan.pieces - 1) * feat : plan.pieces * feat]
@@ -595,40 +711,63 @@
 def main_kernel(
     dims, points, ids, shift, level, w_in, b_in, w_out, inv_scale, freq, phase,
     residual, direction, prior,
-    out_all,
-    feat_all, turned, slabs, outs, right, left, capacity, inverse, basis, send_sem, recv_sem,
+    res_all, dir_all,
+    feat_all, turned, slabs, right, left, capacity, inverse, basis, passed, stage, send_sem, recv_sem,
 ):
     peers = Peers(*dims)
-    me, count = peers.me, peers.count
+    rows, cols = dims
     n, rhs = direction.shape
     feat, rank = freq.shape
     plan = Plan(dims, n, rhs, feat)
-    q, per, wide, windows = plan.q, plan.per, plan.wide, plan.windows
+    count, pairs, q, per = plan.count, plan.pairs, plan.q, plan.per
+    wide, windows = plan.wide, plan.windows
+    r, c = lax.axis_index("row"), lax.axis_index("col")
+    half = lax.rem(r, 2)
+    pair = (r // 2) * cols + c
+    me = half * pairs + pair
     f32 = jnp.float32
+
+    def device(h, p):
+        return {"row": 2 * (p // cols) + h, "col": lax.rem(p, cols)}
+
+    sibling = {"row": 2 * (r // 2) + (1 - half), "col": c}
+
+    def loop(first, body):
+        def step(i, carry):
+            body(lax.rem(pair + i, pairs))
+            return carry
+
+        lax.fori_loop(first, pairs, step, 0)
+
     peers.greet()
     scaled, noise = features(
         points[...], ids[...], shift[...], level[...], w_in[...], b_in[...], w_out[...], inv_scale[...]
     )
     for t, tile in enumerate(pack_tiles(plan, scaled, noise)):
-        feat_all[me, t] = tile
+        feat_all[half, pair, t] = tile
     peers.meet()
-    peers.each(
-        lambda t, dev: peers.send(
-            feat_all.at[me], feat_all.at[me], send_sem.at[0], recv_sem.at[0], dev
-        )
-    )
+    mine = feat_all.at[half, pair]
+    loop(1, lambda p: peers.send(mine, mine, send_sem.at[0], recv_sem.at[0], device(half, p)))
     stacked = jnp.concatenate(
         [direction[...], residual[...], prior[...], jnp.zeros((127 - 2 * n, rhs), f32)], axis=0
     )
     spun = pltpu.roll(stacked.T, n * lax.rem(me, per), 1)
-    for t in range(count):
-        turned[t] = spun[t * q : (t + 1) * q]
-    slabs[me] = turned[me]
-    peers.each(
-        lambda t, dev: peers.send(
-            turned.at[t], slabs.at[me], send_sem.at[1], recv_sem.at[1], dev
-        )
-    )
+    for p in range(pairs):
+        turned[p] = spun[p * q : (p + 1) * q]
+
+    def give(p):
+        peers.send(turned.at[p], slabs.at[me], send_sem.at[2], recv_sem.at[2], device(0, p))
+
+    loop(1, give)
+
+    @pl.when(half == 1)
+    def _():
+        give(pair)
+
+    @pl.when(half == 0)
+    def _():
+        slabs[me] = turned[pair]
+
     turn = 1.0 / (2.0 * math.pi)
     both = jnp.concatenate([freq[...], phase[...], jnp.zeros((127 - feat, rank), f32)], axis=0) * turn
     fp = both.T
@@ -643,110 +782,147 @@
     lane = iota((1, 128), 1)
     live = live_lanes(plan)
 
-    take(feat_all.at[pl.ds(0, count - 1)], recv_sem.at[0])
+    take(feat_all.at[0, pl.ds(0, pairs - 1)], recv_sem.at[0])
+    peers.send(feat_all.at[half], feat_all.at[half], send_sem.at[1], recv_sem.at[1], sibling)
+    take(feat_all.at[0], recv_sem.at[1])
     ft, levels = unpack_tiles(plan, feat_all)
     levels = jnp.where(live, levels, 1.0)
     rsn = jnp.where(live, lax.rsqrt(levels), 0.0)
     h, m, l = split(ft)
-    scale2 = math.log2(math.e)
-    ft2 = ft * scale2
-    h2, m2, l2 = split(ft2)
+    ft2 = ft * math.log2(math.e)
     sq = -0.5 * jnp.sum(ft2 * ft, axis=0, keepdims=True)
     sqs = [p.astype(f32) for p in split(sq)]
     ones = jnp.ones((3, wide), f32)
-    tail = 256 - 6 * feat
-    rest = jnp.zeros((tail - 6, wide), f32)
+    rest = jnp.zeros((256 - 6 * feat - 6, wide), f32)
     right[...] = jnp.concatenate(
         [h, m, l, h, m, h, jnp.concatenate([ones] + sqs + [rest], axis=0).astype(BF16)], axis=0
     )
-    low = jnp.concatenate(
-        [h2, h2, h2, m2, m2, l2, jnp.concatenate(sqs + [ones, rest], axis=0).astype(BF16)], axis=0
-    )
-    left[...] = low.T
     amp = math.sqrt(2.0 / rank)
     u = dot(spectral, right[...])
-    c = cosine_turns(u) * (amp * rsn)
-    ch, cm, cl = split(c)
+    ch, cm, cl = split(cosine_turns(u) * (amp * rsn))
     basis[0] = ch
     basis[1] = cm
     basis[2] = cl
-    diag = iota((rank, rank), 0) == iota((rank, rank), 1)
-    capacity[...] = (
-        jnp.where(diag, 1.0, 0.0)
-        + dot(ch, ch, 1, 1) + (dot(ch, cm, 1, 1) + dot(cm, ch, 1, 1))
-        + (dot(cm, cm, 1, 1) + dot(ch, cl, 1, 1) + dot(cl, ch, 1, 1))
-    )
-    inverse[...] = invert(capacity[...])
-
-    take(slabs.at[pl.ds(0, count - 1)], recv_sem.at[1])
-    zero = jnp.zeros((q, 128), f32)
-    dirs, ress = [], []
-    for w in range(windows):
-        own = [slabs[w * per + k] if w * per + k < count else zero for k in range(per)]
-        d, r = zero, zero
-        for k in range(per):
-            d = jnp.where(between(lane, k * n, n), own[k], d)
-            r = jnp.where(between(lane, (k + 1) * n, n), own[k], r)
-        dirs.append(d)
-        ress.append(pltpu.roll(r, 128 - n, 1))
-    d = jnp.concatenate(dirs, axis=1)
-    r = jnp.concatenate(ress, axis=1)
-    mine = pltpu.roll(slabs[me], 128 - n * lax.rem(me, per), 1)
-    own_prior = mine[:, 2 * n : 2 * n + 1]
-    d3 = rows_of(d)
-    acc = jnp.zeros((d3.shape[0], wide), f32)
-    for w in range(windows):
-        e = dot(left[w * 128 : (w + 1) * 128, :], right[...])
-        k = jnp.exp2(e)
-        kh = k.astype(BF16)
-        kl = (k - kh.astype(f32)).astype(BF16)
-        part = d3[:, w * 128 : (w + 1) * 128]
-        acc = acc + (dot(part, kh) + dot(part, kl))
-    img = fold(acc, q) + levels * d
-    alpha = own_prior / jnp.sum(d * img, axis=1, keepdims=True)
-    nres = r - alpha * img
-    y = nres * rsn
-    y3 = rows_of(y)
-    proj = fold(
-        dot(y3, basis[0], 1, 1) + dot(y3, basis[1], 1, 1) + dot(y3, basis[2], 1, 1), q
-    )
-    coeffs = mm(proj, inverse[...])
-    coeffs = coeffs + mm(proj - mm(coeffs, capacity[...]), inverse[...])
-    c3 = rows_of(coeffs)
-    back = fold(dot(c3, basis[0]) + dot(c3, basis[1]) + dot(c3, basis[2]), q)
-    precond = (y - back) * rsn
-    prod = jnp.sum(nres * precond, axis=1, keepdims=True)
-    ndir = precond + prod / own_prior * d
-    for w in range(windows):
-        part = nres[:, w * 128 : (w + 1) * 128]
-        side = pltpu.roll(ndir[:, w * 128 : (w + 1) * 128], n, 1)
-        for k in range(per):
-            t = w * per + k
-            if t < count:
-                slab = jnp.where(lane == (k * n + 2 * n) % 128, alpha, prod)
-                slab = jnp.where(between(lane, (k + 1) * n, n), side, slab)
-                outs[t] = jnp.where(between(lane, k * n, n), part, slab)
-    out_all[me] = outs[me]
-    peers.each(
-        lambda t, dev: peers.send(outs.at[t], out_all.at[me], send_sem.at[2], recv_sem.at[2], dev)
-    )
-    others = pl.ds(0, count - 1)
-    take(out_all.at[others], recv_sem.at[2])
-    take(feat_all.at[others], send_sem.at[0])
-    take(slabs.at[others], send_sem.at[1])
-    take(out_all.at[others], send_sem.at[2])
-
-
-def finish_kernel(dims, got, direction, sol, new_sol, new_res, new_dir, new_prod):
-    me = lax.axis_index("row") * dims[1] + lax.axis_index("col")
+    tail = lane >= per * n
+
+    @pl.when(half == 0)
+    def _():
+        h2, m2, l2 = split(ft2)
+        low = jnp.concatenate(
+            [h2, h2, h2, m2, m2, l2, jnp.concatenate(sqs + [ones, rest], axis=0).astype(BF16)], axis=0
+        )
+        left[...] = low.T
+        take(slabs.at[pl.ds(0, count - 1)], recv_sem.at[2])
+        zero = jnp.zeros((q, 128), f32)
+        dirs, ress = [], []
+        for w in range(windows):
+            own = [slabs[w * per + k] if w * per + k < count else zero for k in range(per)]
+            d, x = zero, zero
+            for k in range(per):
+                d = jnp.where(between(lane, k * n, n), own[k], d)
+                x = jnp.where(between(lane, (k + 1) * n, n), own[k], x)
+            dirs.append(d)
+            ress.append(pltpu.roll(x, 128 - n, 1))
+        d = jnp.concatenate(dirs, axis=1)
+        res = jnp.concatenate(ress, axis=1)
+        spin = pltpu.roll(slabs[me], lax.rem(128 - n * lax.rem(me, per), 128), 1)
+        own_prior = spin[:, 2 * n : 2 * n + 1]
+        d3 = rows_of(d)
+        acc = jnp.zeros((d3.shape[0], wide), f32)
+        for w in range(windows):
+            k = jnp.exp2(dot(left[w * 128 : (w + 1) * 128, :], right[...]))
+            kh = k.astype(BF16)
+            kl = (k - kh.astype(f32)).astype(BF16)
+            part = d3[:, w * 128 : (w + 1) * 128]
+            acc = acc + (dot(part, kh) + dot(part, kl))
+        img = fold(acc, q) + levels * d
+        alpha = own_prior / jnp.sum(d * img, axis=1, keepdims=True)
+        nres = res - alpha * img
+        y = nres * rsn
+        y3 = rows_of(y)
+        proj = fold(
+            dot(y3, basis[0], 1, 1) + dot(y3, basis[1], 1, 1) + dot(y3, basis[2], 1, 1), q
+        )
+        for w in range(windows):
+            at = slice(w * 128, (w + 1) * 128)
+            stage[w] = jnp.where(tail, alpha, nres[:, at])
+            passed[w] = d[:, at]
+            passed[windows + w] = y[:, at]
+        for w in range(rank // 128):
+            passed[2 * windows + w] = proj[:, w * 128 : (w + 1) * 128]
+        passed[2 * windows + rank // 128] = jnp.broadcast_to(own_prior, (q, 128))
+        peers.send(passed, passed, send_sem.at[3], recv_sem.at[3], sibling)
+        res_all[pair] = stage[me // per]
+
+        def give_rest(h, p):
+            s = h * pairs + p
+            peers.send(stage.at[s // per], res_all.at[pair], send_sem.at[4], recv_sem.at[4], device(h, p))
+
+        loop(1, lambda p: give_rest(0, p))
+        loop(0, lambda p: give_rest(1, p))
+
+    @pl.when(half == 1)
+    def _():
+        diag = iota((rank, rank), 0) == iota((rank, rank), 1)
+        cross = dot(ch, cm, 1, 1) + dot(ch, cl, 1, 1)
+        capacity[...] = (
+            jnp.where(diag, 1.0, 0.0) + (dot(ch, ch, 1, 1) + dot(cm, cm, 1, 1)) + (cross + cross.T)
+        )
+        inverse[...] = invert_panels(capacity[...])
+        take(passed, recv_sem.at[3])
+        proj = jnp.concatenate([passed[2 * windows + w] for w in range(rank // 128)], axis=1)
+        coeffs = mm(proj, inverse[...])
+        coeffs = coeffs + mm(proj - mm(coeffs, capacity[...]), inverse[...])
+        c3 = rows_of(coeffs)
+        back = fold(dot(c3, basis[0]) + dot(c3, basis[1]) + dot(c3, basis[2]), q)
+        d = jnp.concatenate([passed[w] for w in range(windows)], axis=1)
+        y = jnp.concatenate([passed[windows + w] for w in range(windows)], axis=1)
+        own_prior = passed[2 * windows + rank // 128][:, 0:1]
+        gap = y - back
+        prod = jnp.sum(y * gap, axis=1, keepdims=True)
+        ndir = gap * rsn + prod / own_prior * d
+        for w in range(windows):
+            stage[w] = jnp.where(tail, prod, ndir[:, w * 128 : (w + 1) * 128])
+        dir_all[pair] = stage[me // per]
+
+        def give_dir(h, p):
+            s = h * pairs + p
+            peers.send(stage.at[s // per], dir_all.at[pair], send_sem.at[4], recv_sem.at[5], device(h, p))
+
+        loop(1, lambda p: give_dir(1, p))
+        loop(0, lambda p: give_dir(0, p))
+
+    @pl.when(half == 0)
+    def _():
+        take(slabs.at[pl.ds(0, pairs - 1)], send_sem.at[2])
+        take(passed, send_sem.at[3])
+        take(res_all.at[pl.ds(0, pairs - 1)], recv_sem.at[4])
+        take(dir_all, recv_sem.at[5])
+
+    @pl.when(half == 1)
+    def _():
+        take(slabs.at[pl.ds(0, pairs)], send_sem.at[2])
+        take(res_all, recv_sem.at[4])
+        take(dir_all.at[pl.ds(0, pairs - 1)], recv_sem.at[5])
+
+    take(feat_all.at[0, pl.ds(0, pairs - 1)], send_sem.at[0])
+    take(feat_all.at[0], send_sem.at[1])
+    take(slabs.at[pl.ds(0, count - 1)], send_sem.at[4])
+
+
+def finish_kernel(dims, res, dirs, direction, sol, new_sol, new_res, new_dir, new_prod, spare):
+    r, c = lax.axis_index("row"), lax.axis_index("col")
+    me = lax.rem(r, 2) * (dims[0] * dims[1] // 2) + (r // 2) * dims[1] + c
     n = direction.shape[0]
-    per = 128 // n
-    back = lax.rem(128 - n * lax.rem(me, per), 128)
-    x = pltpu.roll(got[...], back, 1).T
-    new_res[...] = x[0:n]
-    new_dir[...] = x[n : 2 * n]
-    new_sol[...] = sol[...] + x[2 * n : 2 * n + 1] * direction[...]
-    new_prod[...] = x[2 * n + 1 : 2 * n + 2]
+    own = pl.ds(pl.multiple_of(n * lax.rem(me, 128 // n), 8), n)
+    x = res[...].T
+    spare[...] = x
+    new_res[...] = spare[own, :]
+    new_sol[...] = sol[...] + x[127:128] * direction[...]
+    z = dirs[...].T
+    spare[...] = z
+    new_dir[...] = spare[own, :]
+    new_prod[...] = z[127:128]
 
 
 def per_device_columns(
@@ -756,28 +932,29 @@
     n, rhs = direction.shape
     feat, rank = frequency.shape
     plan = Plan(dims, n, rhs, feat)
-    count, q, wide = plan.count, plan.q, plan.wide
+    count, pairs, q, wide, windows = plan.count, plan.pairs, plan.q, plan.wide, plan.windows
     f32 = jnp.float32
     sds = jax.ShapeDtypeStruct
     row = lambda v: v.reshape(1, -1)
     dma = pltpu.SemaphoreType.DMA
-    got = pl.pallas_call(
+    res, dirs = pl.pallas_call(
         functools.partial(main_kernel, dims),
-        out_shape=sds((count, q, 128), f32),
+        out_shape=(sds((pairs, q, 128), f32), sds((pairs, q, 128), f32)),
         in_specs=[VMEM] * 13,
-        out_specs=VMEM,
+        out_specs=(VMEM,) * 2,
         scratch_shapes=[
-            pltpu.VMEM((count, plan.tiles, 8, 128), f32),
-            pltpu.VMEM((count, q, 128), f32),
-            pltpu.VMEM((count, q, 128), f32),
+            pltpu.VMEM((2, pairs, plan.tiles, 8, 128), f32),
+            pltpu.VMEM((pairs, q, 128), f32),
             pltpu.VMEM((count, q, 128), f32),
             pltpu.VMEM((256, wide), BF16),
             pltpu.VMEM((wide, 256), BF16),
             pltpu.VMEM((rank, rank), f32),
             pltpu.VMEM((rank, rank), f32),
             pltpu.VMEM((3, rank, wide), BF16),
-            dma((3,)),
-            dma((3,)),
+            pltpu.VMEM((2 * windows + rank // 128 + 1, q, 128), f32),
+            pltpu.VMEM((windows, q, 128), f32),
+            dma((6,)),
+            dma((6,)),
         ],
         compiler_params=pltpu.CompilerParams(collective_id=0, has_side_effects=True),
         name="columns",
@@ -790,10 +967,11 @@
     new_sol, new_res, new_dir, new_prod = pl.pallas_call(
         functools.partial(finish_kernel, dims),
         out_shape=(block, block, block, sds((1, rhs), f32)),
-        in_specs=[VMEM] * 3,
+        in_specs=[VMEM] * 4,
         out_specs=(VMEM,) * 4,
+        scratch_shapes=[pltpu.VMEM((128, rhs), f32)],
         name="finish",
-    )(got.reshape(rhs, 128), direction, solution)
+    )(res.reshape(rhs, 128), dirs.reshape(rhs, 128), direction, solution)
     return new_sol, new_res, new_dir, new_prod.reshape(rhs)
 
 

time: 46 us -> 34.6 us (0.75)
  Pallas kernels: 45.2 us -> 33.7 us
    pallas_call x1, Pallas kernels: 43.5 us -> 32.1 us  [per_device_columns(): pl.pallas_call(functools.partial(main_kernel, dims), out_shape=(sds((pair...]
where the time goes in v2:
time: 34.6 us; the launch traced here: 34.4 us
  Pallas kernels  33.7 us (97%)
  between operations  0.64 us (2%)
    pallas_call x1, Pallas kernels, per_device_columns(): pl.pallas_call(functools.partial(main_kernel, dims), out_shape=(sds((pair...  32.1 us
    pallas_call x1, Pallas kernels, per_device_columns(): pl.pallas_call(functools.partial(finish_kernel, dims), out_shape=(block,...  1.6 us

profile of v2, /device:TPU:0, one launch (start us, length us, event | category | flops | bytes accessed | tf_op | source)
XLA Modules:
  0.0 34.4 jit_solution(3366312582585576496)
XLA Ops:
  0.6 32.1 %columns.1 = (f32[16,8,128]{2,1,0:T(8,128)}, f32[16,8,128]{2,1,0:T(8,128)}) custom-call(f32[40,128]{1,0:T(8,128)} %points.1, s32[1,40]{1,0:T(1,128)} %bitcast.15, f32[64,128]{1,0:T(8,128)} %shift.1, f32[1,64]{1,0:T(1,128)} %bitcast.16, f32[128,256]{1,0:T(8,128)} %w_in.1, f32[1,256]{1,0:T(1,128)} %bitcast.13, f32[32,256]{1,0:T(8,128)} %bitcast.12, ...), custom_call_target="tpu_custom_call" | custom-call | tf_op jit(solution)/shard_map/columns/pallas_call | solution.py:940
  32.8 1.6 %finish.1 = (f32[40,128]{1,0:T(8,128)}, f32[40,128]{1,0:T(8,128)}, f32[40,128]{1,0:T(8,128)}, f32[1,128]{1,0:T(1,128)}) custom-call(f32[128,128]{1,0:T(8,128)} %bitcast.10, f32[128,128]{1,0:T(8,128)} %bitcast.11, f32[40,128]{1,0:T(8,128)} %direction.3, f32[40,128]{1,0:T(8,128)} %sol.1), custom_call_target="tpu_custom_call" | custom-call | tf_op jit(solution)/shard_map/finish/pallas_call | solution.py:967

commit v3 on v2

--- a/solution.py
+++ b/solution.py
@@ -712,7 +712,7 @@
     dims, points, ids, shift, level, w_in, b_in, w_out, inv_scale, freq, phase,
     residual, direction, prior,
     res_all, dir_all,
-    feat_all, turned, slabs, right, left, capacity, inverse, basis, passed, stage, send_sem, recv_sem,
+    feat_all, turned, slabs, right, left, capacity, inverse, basis, passed, stage, send_sem, recv_sem, own_sem,
 ):
     peers = Peers(*dims)
     rows, cols = dims
@@ -734,7 +734,7 @@
 
     def loop(first, body):
         def step(i, carry):
-            body(lax.rem(pair + i, pairs))
+            body(lax.rem(2 * pairs + pair - i, pairs))
             return carry
 
         lax.fori_loop(first, pairs, step, 0)
@@ -757,16 +757,6 @@
 
     def give(p):
         peers.send(turned.at[p], slabs.at[me], send_sem.at[2], recv_sem.at[2], device(0, p))
-
-    loop(1, give)
-
-    @pl.when(half == 1)
-    def _():
-        give(pair)
-
-    @pl.when(half == 0)
-    def _():
-        slabs[me] = turned[pair]
 
     turn = 1.0 / (2.0 * math.pi)
     both = jnp.concatenate([freq[...], phase[...], jnp.zeros((127 - feat, rank), f32)], axis=0) * turn
@@ -784,6 +774,16 @@
 
     take(feat_all.at[0, pl.ds(0, pairs - 1)], recv_sem.at[0])
     peers.send(feat_all.at[half], feat_all.at[half], send_sem.at[1], recv_sem.at[1], sibling)
+    loop(1, give)
+
+    @pl.when(half == 1)
+    def _():
+        give(pair)
+
+    @pl.when(half == 0)
+    def _():
+        slabs[me] = turned[pair]
+
     take(feat_all.at[0], recv_sem.at[1])
     ft, levels = unpack_tiles(plan, feat_all)
     levels = jnp.where(live, levels, 1.0)
@@ -852,7 +852,8 @@
             passed[2 * windows + w] = proj[:, w * 128 : (w + 1) * 128]
         passed[2 * windows + rank // 128] = jnp.broadcast_to(own_prior, (q, 128))
         peers.send(passed, passed, send_sem.at[3], recv_sem.at[3], sibling)
-        res_all[pair] = stage[me // per]
+        keep = pltpu.make_async_copy(stage.at[me // per], res_all.at[pair], own_sem.at[0])
+        keep.start()
 
         def give_rest(h, p):
             s = h * pairs + p
@@ -860,6 +861,7 @@
 
         loop(1, lambda p: give_rest(0, p))
         loop(0, lambda p: give_rest(1, p))
+        keep.wait()
 
     @pl.when(half == 1)
     def _():
@@ -871,9 +873,9 @@
         inverse[...] = invert_panels(capacity[...])
         take(passed, recv_sem.at[3])
         proj = jnp.concatenate([passed[2 * windows + w] for w in range(rank // 128)], axis=1)
-        coeffs = mm(proj, inverse[...])
-        coeffs = coeffs + mm(proj - mm(coeffs, capacity[...]), inverse[...])
-        c3 = rows_of(coeffs)
+        p3 = rows_of(proj)
+        ih, im, il = split(inverse[...])
+        c3 = rows_of(fold(dot(p3, ih) + dot(p3, im) + dot(p3, il), q))
         back = fold(dot(c3, basis[0]) + dot(c3, basis[1]) + dot(c3, basis[2]), q)
         d = jnp.concatenate([passed[w] for w in range(windows)], axis=1)
         y = jnp.concatenate([passed[windows + w] for w in range(windows)], axis=1)
@@ -883,7 +885,8 @@
         ndir = gap * rsn + prod / own_prior * d
         for w in range(windows):
             stage[w] = jnp.where(tail, prod, ndir[:, w * 128 : (w + 1) * 128])
-        dir_all[pair] = stage[me // per]
+        keep = pltpu.make_async_copy(stage.at[me // per], dir_all.at[pair], own_sem.at[0])
+        keep.start()
 
         def give_dir(h, p):
             s = h * pairs + p
@@ -891,6 +894,7 @@
 
         loop(1, lambda p: give_dir(1, p))
         loop(0, lambda p: give_dir(0, p))
+        keep.wait()
 
     @pl.when(half == 0)
     def _():
@@ -941,7 +945,7 @@
         functools.partial(main_kernel, dims),
         out_shape=(sds((pairs, q, 128), f32), sds((pairs, q, 128), f32)),
         in_specs=[VMEM] * 13,
-        out_specs=(VMEM,) * 2,
+        out_specs=(pl.BlockSpec(memory_space=pltpu.HBM),) * 2,
         scratch_shapes=[
             pltpu.VMEM((2, pairs, plan.tiles, 8, 128), f32),
             pltpu.VMEM((pairs, q, 128), f32),
@@ -955,6 +959,7 @@
             pltpu.VMEM((windows, q, 128), f32),
             dma((6,)),
             dma((6,)),
+            dma((1,)),
         ],
         compiler_params=pltpu.CompilerParams(collective_id=0, has_side_effects=True),
         name="columns",

time: 34.6 us -> 31.8 us (0.919)
  Pallas kernels: 33.7 us -> 31 us
    pallas_call x1, Pallas kernels: 32.1 us -> 29.4 us  [per_device_columns(): pl.pallas_call(functools.partial(main_kernel, dims), out_shape=(sds((pair...]
where the time goes in v3:
time: 31.8 us; the launch traced here: 31.6 us
  Pallas kernels  31 us (97%)
  between operations  0.64 us (2%)
    pallas_call x1, Pallas kernels, per_device_columns(): pl.pallas_call(functools.partial(main_kernel, dims), out_shape=(sds((pair...  29.4 us
    pallas_call x1, Pallas kernels, per_device_columns(): pl.pallas_call(functools.partial(finish_kernel, dims), out_shape=(block,...  1.6 us

profile of v3, /device:TPU:0, one launch (start us, length us, event | category | flops | bytes accessed | tf_op | source)
XLA Modules:
  0.0 31.6 jit_solution(15723815200114160150)
XLA Ops:
  0.6 29.4 %columns.1 = (f32[16,8,128]{2,1,0:T(8,128)}, f32[16,8,128]{2,1,0:T(8,128)}) custom-call(f32[40,128]{1,0:T(8,128)} %points.1, s32[1,40]{1,0:T(1,128)} %bitcast.15, f32[64,128]{1,0:T(8,128)} %shift.1, f32[1,64]{1,0:T(1,128)} %bitcast.16, f32[128,256]{1,0:T(8,128)} %w_in.1, f32[1,256]{1,0:T(1,128)} %bitcast.13, f32[32,256]{1,0:T(8,128)} %bitcast.12, ...), custom_call_target="tpu_custom_call" | custom-call | tf_op jit(solution)/shard_map/columns/pallas_call | solution.py:944
  30.0 1.6 %finish.1 = (f32[40,128]{1,0:T(8,128)}, f32[40,128]{1,0:T(8,128)}, f32[40,128]{1,0:T(8,128)}, f32[1,128]{1,0:T(1,128)}) custom-call(f32[128,128]{1,0:T(8,128)} %bitcast.10, f32[128,128]{1,0:T(8,128)} %bitcast.11, f32[40,128]{1,0:T(8,128)} %direction.3, f32[40,128]{1,0:T(8,128)} %sol.1), custom_call_target="tpu_custom_call" | custom-call | tf_op jit(solution)/shard_map/finish/pallas_call | solution.py:972
